TPU v7x, 32 devices: a whole 2x2x4 slice. The times are simulated.
32 devices in a mesh: row: 4 (over z), col: 8 (over y, x, core).
Axes of the slice: x: 2, y: 2, z: 4, core: 2. Of those that a mesh axis runs over, the one named last changes fastest.
Arguments:
- points_rhs: bfloat16 [262144, 16], P(('row', 'col')), may hold values from -6 to 6
- leaf_basis: bfloat16 [1024, 256, 64], P(('row', 'col')), may hold values from -0.375 to 0.375
- near_src: int32 [1024, 2], P(('row', 'col')), may hold values from -1 to 1023, as said below
- near_blocks: bfloat16 [1024, 2, 256, 256], P(('row', 'col')), may hold values from -0.25 to 0.25
- transfer_first: bfloat16 [1024, 64, 64], P(('row', 'col')), may hold values from -0.5 to 0.5
- transfer_second: bfloat16 [512, 64, 64], P(('row', 'col')), may hold values from -0.5 to 0.5
- transfer_third: bfloat16 [256, 64, 64], P(('row', 'col')), may hold values from -0.5 to 0.5
- far_zero: int32 [1024, 8], P(('row', 'col')), may hold values from -1 to 1023, as said below
- far_one: int32 [512, 8], P(('row', 'col')), may hold values from -1 to 511, as said below
- far_two: int32 [256, 8], P(('row', 'col')), may hold values from -1 to 255, as said below
- far_three: int32 [128, 8], P(('row', 'col')), may hold values from -1 to 127, as said below
- couple_zero: bfloat16 [1024, 8, 64, 64], P(('row', 'col')), may hold values from -0.25 to 0.25
- couple_one: bfloat16 [512, 8, 64, 64], P(('row', 'col')), may hold values from -0.25 to 0.25
- couple_two: bfloat16 [256, 8, 64, 64], P(('row', 'col')), may hold values from -0.25 to 0.25
- couple_three: bfloat16 [128, 8, 64, 64], P(('row', 'col')), may hold values from -0.25 to 0.25
Outputs:
- product: bfloat16 [262144, 16], P(('row', 'col'))
Inputs may be any that keep to these rules, and one draw needn't show every extreme that they name: `near_src`: each entry is -1 or a leaf whose index differs from its row's by at most 2; -1 only where that leaf would lie outside the grid. `far_zero`: each row has 7 or 8 live entries, first in the row; a live entry of leaf i lies in the same aligned block of 256 leaves as i. `far_one`: each row has 7 or 8 live entries, first in the row; a live entry of cluster i lies in the same aligned block of 128 clusters as i. `far_two`: each row has 7 or 8 live entries, first in the row; a live entry of cluster i lies in the same aligned block of 64 clusters as i. `far_three`: each row has 7 or 8 live entries, first in the row; live entries may name any cluster of the level.
All inputs are finite; a program needn't handle non-finite values.
Results may differ from a plain program's by a relative error of at most 0.0044.
Values may be sent and summed in bfloat16 or wider, within the bound.
No kernel may reach another device: no remote copies, remote signals or barrier semaphores. Data moves between devices by JAX's collectives and lax.ppermute only.
A program may use at most 128 MiB of HBM per device.

v0:
```python
import jax
import jax.numpy as jnp
from jax import lax
from jax.sharding import PartitionSpec as P

LEAF = 256
RANK = 64
NRHS = 16
TOP_LEVEL = lax.Precision.HIGHEST


def padded_2(cells, sides, width):
    for axis, dim in sides:
        count = lax.axis_size(axis)
        ends = count - 1
        head = lax.slice_in_dim(cells, 0, width, axis=dim)
        tail = lax.slice_in_dim(cells, cells.shape[dim] - width, cells.shape[dim], axis=dim)
        cells = jnp.concatenate(
            [
                lax.ppermute(tail, axis, [(i, (i + 1) % count) for i in range(ends)]),
                cells,
                lax.ppermute(head, axis, [((i + 1) % count, i) for i in range(ends)]),
            ],
            axis=dim,
        )
    return cells


def gather_active(table, local_ids, sources):
    is_live = sources >= 0
    selected_rows = jnp.take(table, jnp.clip(local_ids, 0, table.shape[0] - 1), axis=0)
    return jnp.where(is_live[:, :, None, None], selected_rows, jnp.zeros_like(selected_rows))


def couple_level(table, group_start, sources, coupling_block):
    selected_rows = gather_active(table, sources - group_start, sources)
    return jnp.einsum(
        "enyd,endc->eyc", coupling_block, selected_rows, preferred_element_type=jnp.float32
    )


def collect_group(skeleton):
    return lax.all_gather(skeleton, "col", axis=0, tiled=True)


def shards(
    points_rhs,
    leaf_basis,
    near_src,
    near_blocks,
    transfer_first,
    transfer_second,
    transfer_third,
    far_zero,
    far_one,
    far_two,
    far_three,
    couple_zero,
    couple_one,
    couple_two,
    couple_three,
):
    leaf_count = leaf_basis.shape[0]
    leaf_x = points_rhs.reshape(leaf_count, LEAF, NRHS)
    padded = padded_2(points_rhs.reshape(leaf_count, LEAF * NRHS), ((("row", "col"), 0),), 2)
    padded = padded.reshape(leaf_count + 4, LEAF, NRHS)
    skel_zero = jnp.einsum(
        "lpa,lpr->lar", leaf_basis, leaf_x, preferred_element_type=jnp.float32
    ).astype(jnp.bfloat16)
    skeletons = [skel_zero]
    transfers = [transfer_first, transfer_second, transfer_third]
    for transfer in transfers:
        child_skel = skeletons[-1]
        lifted = jnp.einsum(
            "cab,car->cbr", transfer, child_skel, preferred_element_type=jnp.float32
        )
        lifted = lifted.reshape(lifted.shape[0] // 2, 2, RANK, NRHS).sum(axis=1)
        skeletons.append(lifted.astype(jnp.bfloat16))
    tables = [collect_group(skeletons[level_index]) for level_index in range(3)]
    coarse_group = lax.all_gather(skeletons[3], "col", axis=0, tiled=True)
    coarse_table = lax.all_gather(coarse_group, "row", axis=0, tiled=True)
    row_index = lax.axis_index("row")
    lists = [far_zero, far_one, far_two]
    coupling_blocks = [couple_zero, couple_one, couple_two]
    coupled_field = []
    for level_index in range(3):
        group_start = row_index * tables[level_index].shape[0]
        coupled_field.append(
            couple_level(
                tables[level_index], group_start, lists[level_index], coupling_blocks[level_index]
            )
        )
    coupled_field.append(couple_level(coarse_table, 0, far_three, couple_three))
    downward_field = coupled_field[3]
    for level_index in (3, 2, 1):
        spread = jnp.repeat(downward_field, 2, axis=0)
        downward_field = coupled_field[level_index - 1] + jnp.einsum(
            "cab,cbr->car",
            transfers[level_index - 1].astype(jnp.float32),
            spread,
            precision=TOP_LEVEL,
        )
    far_out = jnp.einsum(
        "lpa,lar->lpr", leaf_basis.astype(jnp.float32), downward_field, precision=TOP_LEVEL
    )
    first_leaf = lax.axis_index(("row", "col")) * leaf_count
    near_picked = gather_active(padded, near_src - first_leaf + 2, near_src)
    near_out = jnp.einsum(
        "iknm,ikmr->inr", near_blocks, near_picked, preferred_element_type=jnp.float32
    )
    return (far_out + near_out).reshape(leaf_count * LEAF, NRHS).astype(jnp.bfloat16)


def solution(mesh):
    return jax.shard_map(
        shards,
        mesh=mesh,
        in_specs=(
            P(("row", "col"), None),
            P(("row", "col"), None, None),
            P(("row", "col"), None),
            P(("row", "col"), None, None, None),
            P(("row", "col"), None, None),
            P(("row", "col"), None, None),
            P(("row", "col"), None, None),
            P(("row", "col"), None),
            P(("row", "col"), None),
            P(("row", "col"), None),
            P(("row", "col"), None),
            P(("row", "col"), None, None, None),
            P(("row", "col"), None, None, None),
            P(("row", "col"), None, None, None),
            P(("row", "col"), None, None, None),
        ),
        out_specs=P(("row", "col"), None),
        check_vma=False,
    )
```

profile of v0, /device:TPU:0, one launch (start us, length us, event | category | flops | bytes accessed | tf_op | source)
XLA Modules:
  0.0 106.1 jit_solution(7011895499649475544)
XLA Ops:
  0.0 0.0 copy-start
  0.0 0.0 copy-start.9
  0.0 0.9 fusion.44
  0.9 0.1 copy.67
  1.0 0.8 slice.13
  1.8 3.0 %collective-permute-start = (bf16[2,4096]{1,0:T(2,128)(2,1)}, bf16[2,4096]{1,0:T(2,128)(2,1)}, u32[]{:S(2)}, u32[]{:S(2)}) collective-permute-start(bf16[2,4096]{1,0:T(2,128)(2,1)} %slice.13), channel_id=1, source_target_pairs={{0,1},{1,2},{2,3},{3,4},{4,5},{5,6},{6,7},{7,8},{8,9},{9,10},{10,1... | collective-permute-start | bytes 49160 | tf_op jit(solution)/shard_map/ppermute | solution.py:20
  4.8 0.1 copy.68
  4.9 0.8 slice.15
  5.7 1.3 %collective-permute-start.1 = (bf16[2,4096]{1,0:T(2,128)(2,1)}, bf16[2,4096]{1,0:T(2,128)(2,1)}, u32[]{:S(2)}, u32[]{:S(2)}) collective-permute-start(bf16[2,4096]{1,0:T(2,128)(2,1)} %slice.15), channel_id=1, source_target_pairs={{1,0},{2,1},{3,2},{4,3},{5,4},{6,5},{7,6},{8,7},{9,8},{10,9},{11,1... | collective-permute-start | bytes 49160 | tf_op jit(solution)/shard_map/ppermute | solution.py:22
  7.0 0.7 compare_select_fusion.3
  7.7 1.3 %broadcast_compare_fusion.3 = (pred[4,8]{1,0:T(4,128)(4,1)}, pred[4,8]{1,0:T(4,128)(4,1)}) fusion(s32[4,8]{1,0:T(4,128)} %param.25), kind=kLoop, calls=%fused_computation.72 | loop fusion | flops 256 | bytes 192 | tf_op jit(solution)/shard_map/ge | solution.py:30
  8.9 1.3 %compare_and_fusion = (pred[8,8]{1,0:T(8,128)(4,1)}, s32[8,8]{1,0:T(8,128)S(1)}, pred[8,8]{1,0:T(8,128)(4,1)}) fusion(s32[8,8]{1,0:T(8,128)} %param.24, s32[]{:T(128)S(6)} %mul.17), kind=kLoop, calls=%fused_computation.64 | loop fusion | flops 576 | bytes 644 | tf_op jit(solution)/shard_map/jit(_take)/and | solution.py:31
  10.2 0.1 reshape.86
  10.3 1.6 %convolution_convert_fusion = bf16[32,64,16]{1,2,0:T(8,128)(2,1)S(1)} fusion(bf16[32,256,64]{1,2,0:T(8,128)(2,1)} %param.16, bf16[2,32,8,256]{3,2,1,0:T(8,128)(2,1)} %bitcast.75), kind=kOutput, calls=%fused_computation.11 | convolution fusion | flops 16809984 | bytes 1376256 | tf_op jit(solution)/shard_map/lpa,lpr->lar/dot_general | solution.py:67
  11.9 14.6 %all_gather.15 = bf16[256,64,16]{1,2,0:T(8,128)(2,1)S(1)} all-gather(bf16[32,64,16]{1,2,0:T(8,128)(2,1)S(1)} %convolution_convert_fusion), channel_id=1, replica_groups=mesh['row'=4,'col'=8] {'col'}, dimensions={0}, use_global_device_ids=true | all-gather | bytes 589824 | tf_op jit(solution)/shard_map/all_gather | solution.py:43
  26.6 1.3 %bitcast_reduce_fusion = bf16[16,64,16]{1,2,0:T(8,128)(2,1)S(1)} fusion(bf16[32,64,16]{1,2,0:T(8,128)(2,1)S(1)} %convolution_convert_fusion, bf16[32,64,64]{2,1,0:T(8,128)(2,1)} %param.19), kind=kOutput, calls=%fused_computation.35 | convolution fusion | flops 4210688 | bytes 360448 | tf_op jit(solution)/shard_map/cab,car->cbr/dot_general | solution.py:74
  27.9 10.0 %all_gather.16 = bf16[128,64,16]{1,2,0:T(8,128)(2,1)} all-gather(bf16[16,64,16]{1,2,0:T(8,128)(2,1)S(1)} %bitcast_reduce_fusion), channel_id=1, replica_groups=mesh['row'=4,'col'=8] {'col'}, dimensions={0}, use_global_device_ids=true | all-gather | bytes 294912 | tf_op jit(solution)/shard_map/all_gather | solution.py:43
  37.8 0.2 bitcast_reduce_fusion.1
  38.0 9.2 %all_gather.17 = bf16[64,64,16]{1,2,0:T(8,128)(2,1)S(1)} all-gather(bf16[8,64,16]{1,2,0:T(8,128)(2,1)S(1)} %bitcast_reduce_fusion.1), channel_id=1, replica_groups=mesh['row'=4,'col'=8] {'col'}, dimensions={0}, use_global_device_ids=true | all-gather | bytes 147456 | tf_op jit(solution)/shard_map/all_gather | solution.py:43
  47.2 0.1 bitcast_reduce_fusion.2
  47.4 8.3 %all_gather.18 = bf16[32,64,16]{1,2,0:T(8,128)(2,1)S(1)} all-gather(bf16[4,64,16]{1,2,0:T(8,128)(2,1)S(1)} %bitcast_reduce_fusion.2), channel_id=1, replica_groups=mesh['row'=4,'col'=8] {'col'}, dimensions={0}, use_global_device_ids=true | all-gather | bytes 73728 | tf_op jit(solution)/shard_map/all_gather | solution.py:80
  55.7 17.5 %all_gather.19 = bf16[128,64,16]{1,2,0:T(8,128)(2,1)} all-gather(bf16[32,64,16]{1,2,0:T(8,128)(2,1)S(1)} %all_gather.18), channel_id=1, replica_groups=mesh['row'=4,'col'=8] {'row'}, dimensions={0}, use_global_device_ids=true | all-gather | bytes 327680 | tf_op jit(solution)/shard_map/all_gather | solution.py:81
  73.2 0.1 reshape.94
  73.3 0.1 copy.64
  73.4 0.1 reshape.78
  73.5 0.7 copy.62
  74.1 0.7 copy.63
  74.8 0.0 copy-done.9
  74.8 0.1 copy.61
  74.9 0.1 reshape.70
  75.0 0.1 copy.58
  75.1 0.7 copy.59
  75.8 1.3 %compare_and_fusion.3 = (pred[32,2]{0,1:T(4,128)(4,1)}, s32[32,2]{0,1:T(2,128)S(1)}, pred[32,2]{0,1:T(4,128)(4,1)}) fusion(s32[32,2]{0,1:T(2,128)} %param.17, s32[]{:T(128)S(6)} %mul.19), kind=kLoop, calls=%fused_computation.70 | loop fusion | flops 640 | bytes 644 | tf_op jit(solution)/shard_map/jit(_take)/and | solution.py:31
  77.0 0.1 copy.72
  77.1 0.7 reshape.102
  77.8 1.3 %gather_fusion.2 = bf16[64,64,16]{1,2,0:T(8,128)(2,1)} fusion(bf16[64,64,16]{1,2,0:T(8,128)(2,1)S(1)} %all_gather.17, s32[1024]{0:T(1024)S(1)} %pad_clamp_fusion.2), kind=kCustom, calls=%fused_computation.2 | custom fusion | bytes 262400 | tf_op jit(solution)/shard_map/jit(_take)/gather | solution.py:31
  79.1 1.6 %gather_fusion.3 = bf16[32,64,16]{1,2,0:T(8,128)(2,1)S(1)} fusion(bf16[128,64,16]{1,2,0:T(8,128)(2,1)} %all_gather.19, s32[1024]{0:T(1024)S(1)} %pad_clamp_fusion.1), kind=kCustom, calls=%fused_computation.3 | custom fusion | bytes 131200 | tf_op jit(solution)/shard_map/jit(_take)/gather | solution.py:31
  80.8 1.8 %convolution_bitcast_fusion.3 = f32[8,16,64]{2,1,0:T(8,128)S(1)} fusion(bf16[8,8,64,64]{3,2,1,0:T(8,128)(2,1)} %param.28, bf16[8,8,64,16]{2,3,1,0:T(8,128)(2,1)} %bitcast.73, pred[8,8]{1,0:T(8,128)(4,1)} %get-tuple-element.5, pred[8,8]{1,0:T(8,128)(4,1)} %get-tuple-element.15), kind=kOutput, calls=%fused_computation.17 | convolution fusion | flops 8519680 | bytes 688256 | tf_op jit(solution)/shard_map/enyd,endc->eyc/dot_general | solution.py:37
  82.5 1.4 %convolution_bitcast_fusion.4 = f32[4,64,16]{1,2,0:T(8,128)S(1)} fusion(bf16[4,8,64,64]{3,2,1,0:T(8,128)(2,1)} %param.29, bf16[4,8,64,16]{2,3,1,0:T(8,128)(2,1)S(1)} %bitcast.74, pred[4,8]{1,0:T(4,128)(4,1)} %get-tuple-element.19, pred[4,8]{1,0:T(4,128)(4,1)} %get-tuple-element.18), kind=kOutput, calls=%fused_computation.18 | convolution fusion | flops 4259840 | bytes 344128 | tf_op jit(solution)/shard_map/enyd,endc->eyc/dot_general | solution.py:37
  84.0 1.2 %fusion.3 = f32[8,64,16]{1,2,0:T(8,128)S(1)} fusion(f32[8,16,64]{2,1,0:T(8,128)S(1)} %convolution_bitcast_fusion.3, f32[8,64,16]{1,2,0:T(8,128)S(1)} %bitcast.80, bf16[8,64,64]{2,1,0:T(8,128)(2,1)} %param.21), kind=kOutput, calls=%fused_computation.16 | convolution fusion | flops 6299648 | bytes 163840 | tf_op jit(solution)/shard_map/cab,cbr->car/dot_general | solution.py:97
  85.2 2.5 %gather_fusion.1 = bf16[128,64,16]{1,2,0:T(8,128)(2,1)} fusion(bf16[128,64,16]{1,2,0:T(8,128)(2,1)} %all_gather.16, s32[1024]{0:T(1024)S(1)} %pad_clamp_fusion.3), kind=kCustom, calls=%fused_computation.1 | custom fusion | bytes 524800 | tf_op jit(solution)/shard_map/jit(_take)/gather | solution.py:31
  87.7 0.0 copy-done.13
  87.7 1.8 %convolution_bitcast_fusion.2 = f32[16,16,64]{2,1,0:T(8,128)S(1)} fusion(bf16[16,8,64,64]{3,2,1,0:T(8,128)(2,1)S(1)} %copy-done, bf16[16,8,64,16]{2,3,1,0:T(8,128)(2,1)} %bitcast.72, pred[16,8]{1,0:T(8,128)(4,1)} %copy.63, pred[16,8]{1,0:T(8,128)(4,1)S(1)} %copy-done.13), kind=kOutput, calls=%fused_computation.14 | convolution fusion | flops 17039360 | bytes 1376512 | tf_op jit(solution)/shard_map/enyd,endc->eyc/dot_general | solution.py:37
  89.5 0.5 fusion.2
  90.0 1.8 %gather_fusion = bf16[256,64,16]{1,2,0:T(8,128)(2,1)} fusion(bf16[256,64,16]{1,2,0:T(8,128)(2,1)S(1)} %all_gather.15, s32[1024]{0:T(1024)S(1)} %pad_clamp_fusion.4), kind=kCustom, calls=%fused_computation | custom fusion | bytes 1049600 | tf_op jit(solution)/shard_map/jit(_take)/gather | solution.py:31
  91.8 3.3 %convolution_bitcast_fusion.1 = f32[32,16,64]{2,1,0:T(8,128)S(1)} fusion(bf16[32,8,64,64]{3,2,1,0:T(8,128)(2,1)} %param.26, bf16[32,8,64,16]{2,3,1,0:T(8,128)(2,1)} %bitcast.71, pred[32,8]{1,0:T(8,128)(4,1)S(1)} %copy-done.7, pred[32,8]{1,0:T(8,128)(4,1)S(1)} %copy.58), kind=kOutput, calls=%fused_computation.9 | convolution fusion | flops 34078720 | bytes 2753024 | tf_op jit(solution)/shard_map/enyd,endc->eyc/dot_general | solution.py:37
  95.2 0.9 convolution_add_fusion.1
  96.2 0.0 copy-done.12
  96.2 0.0 copy-done.3
  96.2 0.0 copy-done.11
  96.2 0.1 copy.65
  96.3 0.1 copy.66
  96.4 0.0 collective-permute-done
  96.4 0.9 concatenate.8
  97.3 0.1 copy.69
  97.4 0.0 collective-permute-done.1
  97.4 0.9 concatenate.9
  98.3 0.1 copy.71
  98.4 0.6 gather_fusion.4
  99.0 0.0 copy-start.1
  99.0 5.8 %convolution_bitcast_fusion = f32[32,16,256]{2,1,0:T(8,128)S(1)} fusion(bf16[32,2,256,256]{3,2,1,0:T(8,128)(2,1)} %param.18, bf16[32,2,256,16]{2,3,1,0:T(8,128)(2,1)S(1)} %bitcast.70, pred[32,2]{1,0:T(8,128)(4,1)S(1)} %copy.66, pred[32,2]{1,0:T(8,128)(4,1)S(1)} %copy.65), kind=kOutput, calls=%fused_computation.6 | convolution fusion | flops 134742016 | bytes 9437312 | tf_op jit(solution)/shard_map/iknm,ikmr->inr/dot_general | solution.py:108
  104.8 0.0 copy-done.1
  104.8 0.6 fusion.1
  105.4 0.7 copy.80
  (31 shorter events, 0.2 us)
Async XLA Ops:
  0.0 87.7 %copy-start = (bf16[16,8,64,64]{3,2,1,0:T(8,128)(2,1)S(1)}, bf16[16,8,64,64]{3,2,1,0:T(8,128)(2,1)}, u32[]{:S(2)}) copy-start(bf16[16,8,64,64]{3,2,1,0:T(8,128)(2,1)} %param.27) | copy-start | bytes 3145732
  0.0 37.8 %copy-start.4 = (bf16[16,64,64]{2,1,0:T(8,128)(2,1)S(1)}, bf16[16,64,64]{2,1,0:T(8,128)(2,1)}, u32[]{:S(2)}) copy-start(bf16[16,64,64]{2,1,0:T(8,128)(2,1)} %param.20) | copy-start | bytes 393220
  0.0 47.2 %copy-start.6 = (bf16[8,64,64]{2,1,0:T(8,128)(2,1)S(1)}, bf16[8,64,64]{2,1,0:T(8,128)(2,1)}, u32[]{:S(2)}) copy-start(bf16[8,64,64]{2,1,0:T(8,128)(2,1)} %param.21) | copy-start | bytes 196612
  0.0 73.3 %copy-start.8 = (s32[16,8]{0,1:T(8,128)S(1)}, s32[16,8]{0,1:T(8,128)}, u32[]{:S(2)}) copy-start(s32[16,8]{0,1:T(8,128)} %param.23) | copy-start | bytes 1540
  0.0 74.8 %copy-start.9 = (s32[32,8]{0,1:T(8,128)S(1)}, s32[32,8]{0,1:T(8,128)}, u32[]{:S(2)}) copy-start(s32[32,8]{0,1:T(8,128)} %param.22) | copy-start | bytes 3076
  1.8 94.6 %collective-permute-start = (bf16[2,4096]{1,0:T(2,128)(2,1)}, bf16[2,4096]{1,0:T(2,128)(2,1)}, u32[]{:S(2)}, u32[]{:S(2)}) collective-permute-start(bf16[2,4096]{1,0:T(2,128)(2,1)} %slice.13), channel_id=1, source_target_pairs={{0,1},{1,2},{2,3},{3,4},{4,5},{5,6},{6,7},{7,8},{8,9},{9,10},{10,1... | collective-permute-start | bytes 49160 | tf_op jit(solution)/shard_map/ppermute | solution.py:20
  5.7 91.7 %collective-permute-start.1 = (bf16[2,4096]{1,0:T(2,128)(2,1)}, bf16[2,4096]{1,0:T(2,128)(2,1)}, u32[]{:S(2)}, u32[]{:S(2)}) collective-permute-start(bf16[2,4096]{1,0:T(2,128)(2,1)} %slice.15), channel_id=1, source_target_pairs={{1,0},{2,1},{3,2},{4,3},{5,4},{6,5},{7,6},{8,7},{9,8},{10,9},{11,1... | collective-permute-start | bytes 49160 | tf_op jit(solution)/shard_map/ppermute | solution.py:22
  79.1 8.6 %copy-start.13 = (pred[16,8]{1,0:T(8,128)(4,1)S(1)}, pred[16,8]{1,0:T(8,128)(4,1)}, u32[]{:S(2)}) copy-start(pred[16,8]{1,0:T(8,128)(4,1)} %copy.62) | copy-start | bytes 388
  82.5 7.0 %copy-start.5 = (bf16[16,64,64]{2,1,0:T(8,128)(2,1)S(1)}, bf16[16,64,64]{2,1,0:T(8,128)(2,1)}, u32[]{:S(2)}) copy-start(bf16[16,64,64]{2,1,0:T(8,128)(2,1)} %param.20) | copy-start | bytes 393220
  90.0 1.8 %copy-start.7 = (pred[32,8]{1,0:T(8,128)(4,1)S(1)}, pred[32,8]{1,0:T(8,128)(4,1)}, u32[]{:S(2)}) copy-start(pred[32,8]{1,0:T(8,128)(4,1)} %copy.59) | copy-start | bytes 772
  91.8 3.4 %copy-start.2 = (bf16[32,64,64]{2,1,0:T(8,128)(2,1)S(1)}, bf16[32,64,64]{2,1,0:T(8,128)(2,1)}, u32[]{:S(2)}) copy-start(bf16[32,64,64]{2,1,0:T(8,128)(2,1)} %param.19) | copy-start | bytes 786436
  91.8 4.4 %copy-start.12 = (s32[64]{0:T(128)S(1)}, s32[64]{0:T(128)}, u32[]{:S(2)}) copy-start(s32[64]{0:T(128)} %reshape.102) | copy-start | bytes 772
  91.8 4.4 %copy-start.3 = (bf16[8192,16]{0,1:T(8,128)(2,1)S(1)}, bf16[8192,16]{0,1:T(8,128)(2,1)}, u32[]{:S(2)}) copy-start(bf16[8192,16]{0,1:T(8,128)(2,1)} %param.15) | copy-start | bytes 786436
  91.8 4.4 %copy-start.11 = (pred[32,2]{0,1:T(4,128)(4,1)S(1)}, pred[32,2]{0,1:T(4,128)(4,1)}, u32[]{:S(2)}) copy-start(pred[32,2]{0,1:T(4,128)(4,1)} %get-tuple-element.20) | copy-start | bytes 196
  91.8 4.5 %copy-start.10 = (pred[32,2]{0,1:T(4,128)(4,1)S(1)}, pred[32,2]{0,1:T(4,128)(4,1)}, u32[]{:S(2)}) copy-start(pred[32,2]{0,1:T(4,128)(4,1)} %get-tuple-element.11) | copy-start | bytes 196
  99.0 5.8 %copy-start.1 = (bf16[32,256,64]{1,2,0:T(8,128)(2,1)S(1)}, bf16[32,256,64]{1,2,0:T(8,128)(2,1)}, u32[]{:S(2)}) copy-start(bf16[32,256,64]{1,2,0:T(8,128)(2,1)} %param.16) | copy-start | bytes 3145732
where the time goes:
time: 107 us; the launch traced here: 106 us
  blocking collectives  59.6 us (56%)
  matrix products  20.5 us (19%)
  local copies, waits for them, and re-layouts  16.8 us (16%)
  other arithmetic  4.61 us (4%)
  starting transfers between devices  4.27 us (4%)
    all_gather x3, blocking collectives, collect_group(): return lax.all_gather(skeleton, 'col', axis=0, tiled=True)  33.8 us
    all_gather x1, blocking collectives, shards(): coarse_table = lax.all_gather(coarse_group, 'row', axis=0, tiled=True)  17.5 us
    all_gather x1, blocking collectives, shards(): coarse_group = lax.all_gather(skeletons[3], 'col', axis=0, tiled=True)  8.34 us
    dot_general x4, matrix products, couple_level(): jnp.einsum('enyd,endc->eyc', coupling_block, selected_rows, preferred_ele...  8.29 us
    gather x5, local copies, waits for them, and re-layouts, gather_active(): jnp.take(table, jnp.clip(local_ids, 0, table.shape[0] - 1), axis=0)  7.86 us
    dot_general x1, matrix products, shards(): jnp.einsum('iknm,ikmr->inr', near_blocks, near_picked, preferred_element_...  5.76 us
    ppermute x1, starting transfers between devices, padded_2(): lax.ppermute(tail, axis, [(i, (i + 1) % count) for i in range(ends)])  2.99 us
    dot_general x3, matrix products, shards(): jnp.einsum('cab,cbr->car', transfers[level_index - 1].astype(jnp.float32)...  2.64 us
  transfers between devices with their start and end apart: 2, of which 0 were waited for; matrix products, arithmetic and copies ran while one was open for 30% of the time, Pallas kernels for 0%

commit v1 on v0

--- a/solution.py
+++ b/solution.py
@@ -1,3 +1,4 @@
+import functools
 import jax
 import jax.numpy as jnp
 from jax import lax
@@ -7,6 +8,16 @@
 RANK = 64
 NRHS = 16
 TOP_LEVEL = lax.Precision.HIGHEST
+
+
+def expand_matrix_now(view, d_out):
+    heap = []
+    for _ in range(lax.axis_size("col")):
+        heap.append(view)
+    return jnp.concatenate(lax.all_to_all(jnp.stack(heap), "col", 0, 0), axis=d_out)
+
+
+watch_roads_by_axis = functools.partial(expand_matrix_now, d_out=0)
 
 
 def padded_2(cells, sides, width):
@@ -40,7 +51,7 @@
 
 
 def collect_group(skeleton):
-    return lax.all_gather(skeleton, "col", axis=0, tiled=True)
+    return watch_roads_by_axis(skeleton)
 
 
 def shards(

time: 107 us -> 116 us (1.084)
  blocking collectives: 59.6 us -> 28.8 us
  starting transfers between devices: 4.27 us -> 17.2 us
  local copies, waits for them, and re-layouts: 16.8 us -> 28 us
  waiting for transfers between devices: 0.01 us -> 9.57 us
  other arithmetic: 4.61 us -> 8.06 us
  matrix products: 20.5 us -> 22.7 us
    all_gather x3 -> x0, blocking collectives: 33.8 us -> none  [collect_group(): return lax.all_gather(skeleton, 'col', axis=0, tiled=True)]
    all_to_all x0 -> x3, starting transfers between devices: none -> 12.9 us  [expand_matrix_now(): lax.all_to_all(jnp.stack(heap), 'col', 0, 0)]
    all_to_all x0 -> x3, waiting for transfers between devices: none -> 9.56 us  [expand_matrix_now(): lax.all_to_all(jnp.stack(heap), 'col', 0, 0)]
    unnamed x28 -> x37, local copies, waits for them, and re-layouts: 0.06 us -> 9.37 us
    all_gather x1, blocking collectives: 8.34 us -> 11.9 us  [shards(): coarse_group = lax.all_gather(skeletons[3], 'col', axis=0, tiled=True)]
    gather x5, local copies, waits for them, and re-layouts: 7.86 us -> 5.32 us  [gather_active(): jnp.take(table, jnp.clip(local_ids, 0, table.shape[0] - 1), axis=0)]
    ge x3, local copies, waits for them, and re-layouts: 0.85 us -> 2.82 us  [gather_active(): is_live = sources >= 0]
    and x3, local copies, waits for them, and re-layouts: 1.44 us -> 3.38 us  [gather_active(): jnp.take(table, jnp.clip(local_ids, 0, table.shape[0] - 1), axis=0)]
  transfers between devices with their start and end apart: 2 -> 5, of which waited for: 0 -> 2; matrix products, arithmetic and copies ran while one was open for 30% -> 38% of each run, Pallas kernels for 0% -> 0%
where the time goes in v1:
time: 116 us; the launch traced here: 115 us
  blocking collectives  28.8 us (25%)
  local copies, waits for them, and re-layouts  28 us (24%)
  matrix products  22.7 us (20%)
  starting transfers between devices  17.2 us (15%)
  waiting for transfers between devices  9.57 us (8%)
  other arithmetic  8.06 us (7%)
    all_gather x1, blocking collectives, shards(): coarse_table = lax.all_gather(coarse_group, 'row', axis=0, tiled=True)  16.9 us
    all_to_all x3, starting transfers between devices, expand_matrix_now(): lax.all_to_all(jnp.stack(heap), 'col', 0, 0)  12.9 us
    all_gather x1, blocking collectives, shards(): coarse_group = lax.all_gather(skeletons[3], 'col', axis=0, tiled=True)  11.9 us
    all_to_all x3, waiting for transfers between devices, expand_matrix_now(): lax.all_to_all(jnp.stack(heap), 'col', 0, 0)  9.56 us
    unnamed x37, local copies, waits for them, and re-layouts  9.37 us
    dot_general x4, matrix products, couple_level(): jnp.einsum('enyd,endc->eyc', coupling_block, selected_rows, preferred_ele...  8.64 us
    dot_general x1, matrix products, shards(): jnp.einsum('iknm,ikmr->inr', near_blocks, near_picked, preferred_element_...  6.5 us
    gather x5, local copies, waits for them, and re-layouts, gather_active(): jnp.take(table, jnp.clip(local_ids, 0, table.shape[0] - 1), axis=0)  5.32 us
  transfers between devices with their start and end apart: 5, of which 2 were waited for; matrix products, arithmetic and copies ran while one was open for 38% of the time, Pallas kernels for 0%

profile of v1, /device:TPU:0, one launch (start us, length us, event | category | flops | bytes accessed | tf_op | source)
XLA Modules:
  0.0 114.7 jit_solution(11879117641498539146)
XLA Ops:
  0.0 1.8 %convolution_convert_fusion = bf16[32,64,16]{1,2,0:T(8,128)(2,1)S(1)} fusion(bf16[32,256,64]{1,2,0:T(8,128)(2,1)} %param.16, bf16[2,32,8,256]{3,2,1,0:T(8,128)(2,1)} %bitcast.90), kind=kOutput, calls=%fused_computation.11 | convolution fusion | flops 16809984 | bytes 1376256 | tf_op jit(solution)/shard_map/lpa,lpr->lar/dot_general | solution.py:78
  1.8 1.3 %bitcast_reduce_fusion = bf16[16,64,16]{1,2,0:T(8,128)(2,1)S(1)} fusion(bf16[32,64,16]{1,2,0:T(8,128)(2,1)S(1)} %convolution_convert_fusion, bf16[32,64,64]{2,1,0:T(8,128)(2,1)} %param.19), kind=kOutput, calls=%fused_computation.35 | convolution fusion | flops 4210688 | bytes 360448 | tf_op jit(solution)/shard_map/cab,car->cbr/dot_general | solution.py:85
  3.1 1.1 bitcast_reduce_fusion.1
  4.3 0.9 reshape.145
  5.2 5.2 %all-to-all-start.2 = ((bf16[8,2,4096]{2,1,0:T(2,128)(2,1)}), bf16[8,2,4096]{2,1,0:T(2,128)(2,1)}, u32[]{:S(2)}, u32[]{:S(2)}) async-start(bf16[8,2,4096]{2,1,0:T(2,128)(2,1)} %reshape.145), calls=%async_computation.2 | async-start | bytes 262144 | tf_op jit(solution)/shard_map/all_to_all | solution.py:17
  10.4 0.7 fusion.44
  11.1 0.1 copy.88
  11.3 0.8 slice.13
  12.0 3.0 %collective-permute-start = (bf16[2,4096]{1,0:T(2,128)(2,1)}, bf16[2,4096]{1,0:T(2,128)(2,1)}, u32[]{:S(2)}, u32[]{:S(2)}) collective-permute-start(bf16[2,4096]{1,0:T(2,128)(2,1)} %slice.13), channel_id=1, source_target_pairs={{0,1},{1,2},{2,3},{3,4},{4,5},{5,6},{6,7},{7,8},{8,9},{9,10},{10,1... | collective-permute-start | bytes 49160 | tf_op jit(solution)/shard_map/ppermute | solution.py:31
  15.0 0.1 copy.89
  15.2 0.8 slice.15
  15.9 1.3 %collective-permute-start.1 = (bf16[2,4096]{1,0:T(2,128)(2,1)}, bf16[2,4096]{1,0:T(2,128)(2,1)}, u32[]{:S(2)}, u32[]{:S(2)}) collective-permute-start(bf16[2,4096]{1,0:T(2,128)(2,1)} %slice.15), channel_id=1, source_target_pairs={{1,0},{2,1},{3,2},{4,3},{5,4},{6,5},{7,6},{8,7},{9,8},{10,9},{11,1... | collective-permute-start | bytes 49160 | tf_op jit(solution)/shard_map/ppermute | solution.py:33
  17.2 0.7 compare_select_fusion.3
  17.9 1.3 %broadcast_compare_fusion.3 = (pred[4,8]{1,0:T(4,128)(4,1)}, pred[4,8]{1,0:T(4,128)(4,1)}) fusion(s32[4,8]{1,0:T(4,128)} %param.25), kind=kLoop, calls=%fused_computation.72 | loop fusion | flops 256 | bytes 192 | tf_op jit(solution)/shard_map/ge | solution.py:41
  19.2 0.9 broadcast_bitcast_fusion.1
  20.0 0.1 broadcast_bitcast_fusion
  20.2 0.6 compare_and_fusion
  20.8 0.1 reshape.104
  20.9 1.1 bitcast_reduce_fusion.2
  22.0 11.9 %all_gather.6 = bf16[32,64,16]{1,2,0:T(8,128)(2,1)S(1)} all-gather(bf16[4,64,16]{1,2,0:T(8,128)(2,1)S(1)} %bitcast_reduce_fusion.2), channel_id=1, replica_groups=mesh['row'=4,'col'=8] {'col'}, dimensions={0}, use_global_device_ids=true | all-gather | bytes 73728 | tf_op jit(solution)/shard_map/all_gather | solution.py:91
  33.9 16.9 %all_gather.7 = bf16[128,64,16]{1,2,0:T(8,128)(2,1)} all-gather(bf16[32,64,16]{1,2,0:T(8,128)(2,1)S(1)} %all_gather.6), channel_id=1, replica_groups=mesh['row'=4,'col'=8] {'row'}, dimensions={0}, use_global_device_ids=true | all-gather | bytes 327680 | tf_op jit(solution)/shard_map/all_gather | solution.py:92
  50.8 0.1 reshape.112
  50.9 1.3 %compare_and_fusion.1 = (pred[16,8]{0,1:T(8,128)(4,1)}, s32[16,8]{0,1:T(8,128)S(1)}, pred[16,8]{0,1:T(8,128)(4,1)}) fusion(s32[16,8]{0,1:T(8,128)} %param.23, s32[]{:T(128)S(6)} %mul.16), kind=kLoop, calls=%fused_computation.65 | loop fusion | flops 1152 | bytes 1284 | tf_op jit(solution)/shard_map/jit(_take)/and | solution.py:42
  52.2 0.1 reshape.96
  52.3 1.3 %compare_and_fusion.2 = (pred[32,8]{0,1:T(8,128)(4,1)}, s32[32,8]{0,1:T(8,128)S(1)}, pred[32,8]{0,1:T(8,128)(4,1)}) fusion(s32[32,8]{0,1:T(8,128)} %param.22, s32[]{:T(128)S(6)} %mul.15), kind=kLoop, calls=%fused_computation.66 | loop fusion | flops 2304 | bytes 2564 | tf_op jit(solution)/shard_map/jit(_take)/and | solution.py:42
  53.7 0.1 reshape.88
  53.8 1.3 %compare_and_fusion.3 = (pred[32,2]{0,1:T(4,128)(4,1)}, s32[32,2]{0,1:T(2,128)S(1)}, pred[32,2]{0,1:T(4,128)(4,1)}) fusion(s32[32,2]{0,1:T(2,128)} %param.17, s32[]{:T(128)S(6)} %mul.19), kind=kLoop, calls=%fused_computation.70 | loop fusion | flops 640 | bytes 644 | tf_op jit(solution)/shard_map/jit(_take)/and | solution.py:42
  55.0 0.1 copy.93
  55.1 0.6 reshape.120
  55.7 1.6 %gather_fusion.3 = bf16[32,64,16]{1,2,0:T(8,128)(2,1)S(1)} fusion(bf16[128,64,16]{1,2,0:T(8,128)(2,1)} %all_gather.7, s32[1024]{0:T(1024)S(1)} %pad_clamp_fusion.1), kind=kCustom, calls=%fused_computation.3 | custom fusion | bytes 131200 | tf_op jit(solution)/shard_map/jit(_take)/gather | solution.py:42
  57.4 2.0 %convolution_bitcast_fusion.4 = f32[4,64,16]{1,2,0:T(8,128)} fusion(bf16[4,8,64,64]{3,2,1,0:T(8,128)(2,1)} %param.29, bf16[4,8,64,16]{2,3,1,0:T(8,128)(2,1)S(1)} %bitcast.89, pred[4,8]{1,0:T(4,128)(4,1)} %get-tuple-element.19, pred[4,8]{1,0:T(4,128)(4,1)} %get-tuple-element.18), kind=kOutput, calls=%fused_computation.18 | convolution fusion | flops 4259840 | bytes 344128 | tf_op jit(solution)/shard_map/enyd,endc->eyc/dot_general | solution.py:48
  59.3 0.7 pad_clamp_fusion
  60.0 0.7 copy.104
  60.7 2.1 %reshape.143 = bf16[8,2,8192]{2,1,0:T(2,128)(2,1)} reshape(bf16[8,16,16,64]{3,2,1,0:T(8,128)(2,1)} %broadcast_bitcast_fusion.1) | data formatting | bytes 524288
  62.9 1.3 %copy.83 = pred[16,8]{1,0:T(8,128)(4,1)} copy(pred[16,8]{0,1:T(8,128)(4,1)} %get-tuple-element.16) | data formatting | bytes 256 | tf_op jit(solution)/shard_map/ge | solution.py:41
  64.2 1.3 %copy.84 = pred[16,8]{1,0:T(8,128)(4,1)} copy(pred[16,8]{0,1:T(8,128)(4,1)} %get-tuple-element.7) | data formatting | bytes 256 | tf_op jit(solution)/shard_map/jit(_take)/and | solution.py:42
  65.5 1.5 %reshape.141 = bf16[8,2,16384]{2,1,0:T(2,128)(2,1)} reshape(bf16[8,32,16,64]{3,2,1,0:T(8,128)(2,1)S(1)} %broadcast_bitcast_fusion) | data formatting | bytes 1048576
  67.0 0.7 copy.79
  67.8 1.3 %copy.80 = pred[32,8]{1,0:T(8,128)(4,1)} copy(pred[32,8]{0,1:T(8,128)(4,1)} %get-tuple-element.9) | data formatting | bytes 512 | tf_op jit(solution)/shard_map/jit(_take)/and | solution.py:42
  69.1 0.8 copy.86
  69.9 0.7 copy.87
  70.6 0.9 concatenate.8
  71.5 0.9 concatenate.9
  72.5 1.0 pad_maximum_fusion
  73.5 0.6 gather_fusion.4
  74.1 6.5 %convolution_bitcast_fusion = f32[32,16,256]{2,1,0:T(8,128)} fusion(bf16[32,2,256,256]{3,2,1,0:T(8,128)(2,1)} %param.18, bf16[32,2,256,16]{2,3,1,0:T(8,128)(2,1)S(1)} %bitcast.82, pred[32,2]{1,0:T(8,128)(4,1)S(1)} %copy.87, pred[32,2]{1,0:T(8,128)(4,1)S(1)} %copy.86), kind=kOutput, calls=%fused_computation.6 | convolution fusion | flops 134742016 | bytes 9437312 | tf_op jit(solution)/shard_map/iknm,ikmr->inr/dot_general | solution.py:119
  80.6 3.5 %all-to-all-start.1 = ((bf16[8,2,8192]{2,1,0:T(2,128)(2,1)}), bf16[8,2,8192]{2,1,0:T(2,128)(2,1)S(1)}, u32[]{:S(2)}, u32[]{:S(2)}) async-start(bf16[8,2,8192]{2,1,0:T(2,128)(2,1)} %reshape.143), calls=%async_computation.1 | async-start | bytes 524288 | tf_op jit(solution)/shard_map/all_to_all | solution.py:17
  84.2 1.1 reshape.146
  85.3 0.6 gather_fusion.2
  86.0 1.7 %convolution_bitcast_fusion.3 = f32[8,16,64]{2,1,0:T(8,128)S(1)} fusion(bf16[8,8,64,64]{3,2,1,0:T(8,128)(2,1)} %param.28, bf16[8,8,64,16]{2,3,1,0:T(8,128)(2,1)S(1)} %bitcast.88, pred[8,8]{1,0:T(8,128)(4,1)S(1)} %copy-done.12, pred[8,8]{1,0:T(8,128)(4,1)S(1)} %copy-done.13), kind=kOutput, calls=%fused_computation.17 | convolution fusion | flops 8519680 | bytes 688256 | tf_op jit(solution)/shard_map/enyd,endc->eyc/dot_general | solution.py:48
  87.7 0.3 fusion.3
  88.0 3.1 %all-to-all-done.1 = bf16[8,2,8192]{2,1,0:T(2,128)(2,1)S(1)} async-done(((bf16[8,2,8192]{2,1,0:T(2,128)(2,1)}), bf16[8,2,8192]{2,1,0:T(2,128)(2,1)S(1)}, u32[]{:S(2)}, u32[]{:S(2)}) %all-to-all-start.1) | async-done | bytes 262176 | tf_op jit(solution)/shard_map/all_to_all | solution.py:17
  91.0 4.1 %all-to-all-start = ((bf16[8,2,16384]{2,1,0:T(2,128)(2,1)}), bf16[8,2,16384]{2,1,0:T(2,128)(2,1)}, u32[]{:S(2)}, u32[]{:S(2)}) async-start(bf16[8,2,16384]{2,1,0:T(2,128)(2,1)} %reshape.141), calls=%async_computation | async-start | bytes 1048576 | tf_op jit(solution)/shard_map/all_to_all | solution.py:17
  95.2 0.3 reshape.144
  95.5 0.7 gather_fusion.1
  96.3 1.6 %convolution_bitcast_fusion.2 = f32[16,16,64]{2,1,0:T(8,128)S(1)} fusion(bf16[16,8,64,64]{3,2,1,0:T(8,128)(2,1)S(1)} %copy-done, bf16[16,8,64,16]{2,3,1,0:T(8,128)(2,1)S(1)} %bitcast.86, pred[16,8]{1,0:T(8,128)(4,1)} %copy.84, pred[16,8]{1,0:T(8,128)(4,1)S(1)} %copy-done.11), kind=kOutput, calls=%fused_computation.14 | convolution fusion | flops 17039360 | bytes 1376512 | tf_op jit(solution)/shard_map/enyd,endc->eyc/dot_general | solution.py:48
  97.9 0.5 fusion.2
  98.4 6.5 %all-to-all-done = bf16[8,2,16384]{2,1,0:T(2,128)(2,1)} async-done(((bf16[8,2,16384]{2,1,0:T(2,128)(2,1)}), bf16[8,2,16384]{2,1,0:T(2,128)(2,1)}, u32[]{:S(2)}, u32[]{:S(2)}) %all-to-all-start) | async-done | bytes 524320 | tf_op jit(solution)/shard_map/all_to_all | solution.py:17
  104.9 2.3 %reshape.142 = bf16[8,32,16,64]{3,2,1,0:T(8,128)(2,1)S(1)} reshape(bf16[8,2,16384]{2,1,0:T(2,128)(2,1)} %all-to-all-done) | data formatting | bytes 1048576
  107.2 1.8 %gather_fusion = bf16[256,64,16]{1,2,0:T(8,128)(2,1)} fusion(bf16[256,64,16]{1,2,0:T(8,128)(2,1)S(1)} %bitcast.83, s32[1024]{0:T(1024)S(1)} %pad_clamp_fusion.4), kind=kCustom, calls=%fused_computation | custom fusion | bytes 1049600 | tf_op jit(solution)/shard_map/jit(_take)/gather | solution.py:42
  109.0 3.4 %convolution_bitcast_fusion.1 = f32[32,16,64]{2,1,0:T(8,128)S(1)} fusion(bf16[32,8,64,64]{3,2,1,0:T(8,128)(2,1)} %param.26, bf16[32,8,64,16]{2,3,1,0:T(8,128)(2,1)} %bitcast.84, pred[32,8]{1,0:T(8,128)(4,1)S(1)} %copy-done.9, pred[32,8]{1,0:T(8,128)(4,1)S(1)} %copy.79), kind=kOutput, calls=%fused_computation.9 | convolution fusion | flops 34078720 | bytes 2753024 | tf_op jit(solution)/shard_map/enyd,endc->eyc/dot_general | solution.py:48
  112.5 0.9 convolution_add_fusion.1
  113.4 0.6 fusion.1
  114.0 0.7 copy.101
  (43 shorter events, 0.5 us)
Async XLA Ops:
  0.0 96.3 %copy-start = (bf16[16,8,64,64]{3,2,1,0:T(8,128)(2,1)S(1)}, bf16[16,8,64,64]{3,2,1,0:T(8,128)(2,1)}, u32[]{:S(2)}) copy-start(bf16[16,8,64,64]{3,2,1,0:T(8,128)(2,1)} %param.27) | copy-start | bytes 3145732
  0.0 20.2 %copy-start.10 = (s32[8,8]{1,0:T(8,128)S(1)}, s32[8,8]{1,0:T(8,128)}, u32[]{:S(2)}) copy-start(s32[8,8]{1,0:T(8,128)} %param.24) | copy-start | bytes 772
  0.0 60.0 %copy-start.4 = (bf16[8192,16]{0,1:T(8,128)(2,1)S(1)}, bf16[8192,16]{0,1:T(8,128)(2,1)}, u32[]{:S(2)}) copy-start(bf16[8192,16]{0,1:T(8,128)(2,1)} %param.15) | copy-start | bytes 786436
  4.3 14.9 %copy-start.7 = (bf16[8,64,16]{1,2,0:T(8,128)(2,1)}, bf16[8,64,16]{1,2,0:T(8,128)(2,1)S(1)}, u32[]{:S(2)}) copy-start(bf16[8,64,16]{1,2,0:T(8,128)(2,1)S(1)} %bitcast_reduce_fusion.1) | copy-start | bytes 49156
  5.2 75.4 %all-to-all-start.2 = ((bf16[8,2,4096]{2,1,0:T(2,128)(2,1)}), bf16[8,2,4096]{2,1,0:T(2,128)(2,1)}, u32[]{:S(2)}, u32[]{:S(2)}) async-start(bf16[8,2,4096]{2,1,0:T(2,128)(2,1)} %reshape.145), calls=%async_computation.2 | async-start | bytes 262144 | tf_op jit(solution)/shard_map/all_to_all | solution.py:17
  12.0 58.5 %collective-permute-start = (bf16[2,4096]{1,0:T(2,128)(2,1)}, bf16[2,4096]{1,0:T(2,128)(2,1)}, u32[]{:S(2)}, u32[]{:S(2)}) collective-permute-start(bf16[2,4096]{1,0:T(2,128)(2,1)} %slice.13), channel_id=1, source_target_pairs={{0,1},{1,2},{2,3},{3,4},{4,5},{5,6},{6,7},{7,8},{8,9},{9,10},{10,1... | collective-permute-start | bytes 49160 | tf_op jit(solution)/shard_map/ppermute | solution.py:31
  15.9 55.6 %collective-permute-start.1 = (bf16[2,4096]{1,0:T(2,128)(2,1)}, bf16[2,4096]{1,0:T(2,128)(2,1)}, u32[]{:S(2)}, u32[]{:S(2)}) collective-permute-start(bf16[2,4096]{1,0:T(2,128)(2,1)} %slice.15), channel_id=1, source_target_pairs={{1,0},{2,1},{3,2},{4,3},{5,4},{6,5},{7,6},{8,7},{9,8},{10,9},{11,1... | collective-permute-start | bytes 49160 | tf_op jit(solution)/shard_map/ppermute | solution.py:33
  74.1 11.8 %copy-start.12 = (pred[8,8]{1,0:T(8,128)(4,1)S(1)}, pred[8,8]{1,0:T(8,128)(4,1)}, u32[]{:S(2)}) copy-start(pred[8,8]{1,0:T(8,128)(4,1)} %get-tuple-element.5) | copy-start | bytes 196
  74.1 11.8 %copy-start.13 = (pred[8,8]{1,0:T(8,128)(4,1)S(1)}, pred[8,8]{1,0:T(8,128)(4,1)}, u32[]{:S(2)}) copy-start(pred[8,8]{1,0:T(8,128)(4,1)} %get-tuple-element.15) | copy-start | bytes 196
  80.6 7.0 %copy-start.8 = (f32[4,64,16]{1,2,0:T(8,128)S(1)}, f32[4,64,16]{1,2,0:T(8,128)}, u32[]{:S(2)}) copy-start(f32[4,64,16]{1,2,0:T(8,128)} %convolution_bitcast_fusion.4) | copy-start | bytes 49156
  80.6 7.0 %copy-start.6 = (bf16[8,64,64]{2,1,0:T(8,128)(2,1)S(1)}, bf16[8,64,64]{2,1,0:T(8,128)(2,1)}, u32[]{:S(2)}) copy-start(bf16[8,64,64]{2,1,0:T(8,128)(2,1)} %param.21) | copy-start | bytes 196612
  80.6 10.4 %all-to-all-start.1 = ((bf16[8,2,8192]{2,1,0:T(2,128)(2,1)}), bf16[8,2,8192]{2,1,0:T(2,128)(2,1)S(1)}, u32[]{:S(2)}, u32[]{:S(2)}) async-start(bf16[8,2,8192]{2,1,0:T(2,128)(2,1)} %reshape.143), calls=%async_computation.1 | async-start | bytes 524288 | tf_op jit(solution)/shard_map/all_to_all | solution.py:17
  85.9 10.3 %copy-start.11 = (pred[16,8]{1,0:T(8,128)(4,1)S(1)}, pred[16,8]{1,0:T(8,128)(4,1)}, u32[]{:S(2)}) copy-start(pred[16,8]{1,0:T(8,128)(4,1)} %copy.83) | copy-start | bytes 388
  91.0 13.9 %all-to-all-start = ((bf16[8,2,16384]{2,1,0:T(2,128)(2,1)}), bf16[8,2,16384]{2,1,0:T(2,128)(2,1)}, u32[]{:S(2)}, u32[]{:S(2)}) async-start(bf16[8,2,16384]{2,1,0:T(2,128)(2,1)} %reshape.141), calls=%async_computation | async-start | bytes 1048576 | tf_op jit(solution)/shard_map/all_to_all | solution.py:17
  95.2 2.7 %copy-start.5 = (bf16[16,64,64]{2,1,0:T(8,128)(2,1)S(1)}, bf16[16,64,64]{2,1,0:T(8,128)(2,1)}, u32[]{:S(2)}) copy-start(bf16[16,64,64]{2,1,0:T(8,128)(2,1)} %param.20) | copy-start | bytes 393220
  107.2 1.8 %copy-start.9 = (pred[32,8]{1,0:T(8,128)(4,1)S(1)}, pred[32,8]{1,0:T(8,128)(4,1)}, u32[]{:S(2)}) copy-start(pred[32,8]{1,0:T(8,128)(4,1)} %copy.80) | copy-start | bytes 772
  109.0 3.5 %copy-start.2 = (bf16[32,64,64]{2,1,0:T(8,128)(2,1)S(1)}, bf16[32,64,64]{2,1,0:T(8,128)(2,1)}, u32[]{:S(2)}) copy-start(bf16[32,64,64]{2,1,0:T(8,128)(2,1)} %param.19) | copy-start | bytes 786436
  109.0 4.4 %copy-start.1 = (bf16[32,256,64]{1,2,0:T(8,128)(2,1)S(1)}, bf16[32,256,64]{1,2,0:T(8,128)(2,1)}, u32[]{:S(2)}) copy-start(bf16[32,256,64]{1,2,0:T(8,128)(2,1)} %param.16) | copy-start | bytes 3145732
  109.0 4.4 %copy-start.3 = (f32[32,16,256]{2,1,0:T(8,128)S(1)}, f32[32,16,256]{2,1,0:T(8,128)}, u32[]{:S(2)}) copy-start(f32[32,16,256]{2,1,0:T(8,128)} %convolution_bitcast_fusion) | copy-start | bytes 1572868
